TPU v7x, 32 devices: a whole 2x2x4 slice. The times are simulated.
32 devices in a mesh: dp: 8 (over z, y), mp: 4 (over x, core).
Axes of the slice: x: 2, y: 2, z: 4, core: 2. Of those that a mesh axis runs over, the one named last changes fastest.
Arguments:
- tokens: bfloat16 [32768, 768], P(('dp', 'mp')), may hold values from -6 to 6
- cotangent: bfloat16 [32768, 768], P(('dp', 'mp')), may hold values from -6 to 6
- prompts: float32 [50, 768], replicated, may hold values from -6 to 6
- segments: int32 [32768], P(('dp', 'mp')), may hold values from 0 to 6, as said below
- prompt_slot_index: int32 [32768], P(('dp', 'mp')), may hold values from 0 to 50, as said below
- norm_gain: float32 [2, 768], replicated, may hold values from 0.5 to 1.5
- norm_shift: float32 [2, 768], replicated, may hold values from -2 to 2
- attn_qkv: bfloat16 [3, 768, 768], P(None, ('dp', 'mp')), may hold values from -0.21875 to 0.21875
- attn_bias: float32 [3, 768], replicated, may hold values from -2 to 2
- attn_out: bfloat16 [768, 768], P(('dp', 'mp')), may hold values from -0.625 to 0.625
- mlp_weight: bfloat16 [2, 768, 3072], P(None, 'dp', 'mp'), may hold values from -0.21875 to 0.21875
- mlp_bias_up: float32 [3072], replicated, may hold values from -2 to 2
- mlp_bias_down: float32 [768], replicated, may hold values from -2 to 2
Outputs:
- block_output: bfloat16 [32768, 768], P(('dp', 'mp'))
- input_grad: float32 [32768, 768], P(('dp', 'mp'))
- prompt_grad: float32 [50, 768], replicated
- gain_grad: float32 [2, 768], replicated
- shift_grad: float32 [2, 768], replicated
- qkv_grad: float32 [3, 768, 768], P(None, ('dp', 'mp'))
- attn_bias_grad: float32 [3, 768], replicated
- attn_out_grad: float32 [768, 768], P(('dp', 'mp'))
- mlp_grad: float32 [2, 768, 3072], P(None, 'dp', 'mp')
- up_bias_grad: float32 [3072], replicated
- down_bias_grad: float32 [768], replicated
Inputs may be any that keep to these rules, and one draw needn't show every extreme that they name: Every packed row holds images of one size: from the row's start, as many whole segments of 151, of 247 or of 627 tokens as fit, numbered from 0, then one segment of the remaining tokens. Row 0 holds the smallest images. `prompt_slot_index`: in each image segment, tokens 1 to 50 carry slots 0 to 49; all other tokens carry 50.
All inputs are finite; a program needn't handle non-finite values.
Results may differ from a plain program's by a relative error of at most 0.014.
Values may be sent and summed in bfloat16 or wider, within the bound.
No kernel may reach another device: no remote copies, remote signals or barrier semaphores. Data moves between devices by JAX's collectives and lax.ppermute only.
A program may use at most 256 MiB of HBM per device.

v0:
```python
from functools import partial
import jax
import jax.numpy as jnp
from jax import lax
from jax.sharding import PartitionSpec as P

HEAD_SIZE = 64
NPROMPT = 50
PACKED_ROW_LENGTH = 1024
EPS = 1e-06
HIGHEST = lax.Precision.HIGHEST
MASKED = -1e30


def layer_norm(value_list, gain_row, shift_row):
    centre = jnp.mean(value_list, axis=-1, keepdims=True)
    centred = value_list - centre
    spread = jnp.mean(centred * centred, axis=-1, keepdims=True)
    return centred * lax.rsqrt(spread + EPS) * gain_row + shift_row


def gelu_exact(value_list):
    return jax.nn.gelu(value_list, approximate=False)


def masked_scores(query_tile, key_heads, seg_tile, seg_row, factor):
    scores = (
        jnp.einsum("qhd,khd->hqk", query_tile, key_heads, preferred_element_type=jnp.float32)
        * factor
    )
    allowed = seg_tile[:, None] == seg_row[None, :]
    return jnp.where(allowed[None], scores, MASKED)


def attend_forward(packed, tile_row_list):
    query_heads, key_heads, value_heads, seg_row = packed
    factor = query_heads.shape[2] ** (-0.5)

    def one_tile(tile_number):
        first_row = tile_number * tile_row_list
        query_tile = lax.dynamic_slice_in_dim(query_heads, first_row, tile_row_list, 0)
        seg_tile = lax.dynamic_slice_in_dim(seg_row, first_row, tile_row_list, 0)
        scores = masked_scores(query_tile, key_heads, seg_tile, seg_row, factor)
        row_peak = jnp.max(scores, axis=-1, keepdims=True)
        raised = jnp.exp(scores - row_peak)
        totals_row = jnp.sum(raised, axis=-1, keepdims=True)
        weights = (raised / totals_row).astype(jnp.bfloat16)
        mixed = jnp.einsum("hqk,khd->qhd", weights, value_heads, preferred_element_type=jnp.float32)
        return (mixed.astype(jnp.bfloat16), (row_peak + jnp.log(totals_row))[:, :, 0])

    return lax.map(one_tile, jnp.arange(query_heads.shape[0] // tile_row_list))


def attend_backward(packed, tile_row_list):
    query_heads, key_heads, value_heads, seg_row, log_sums, grad_heads = packed
    length, head_count, head_width = key_heads.shape
    factor = head_width ** (-0.5)

    def one_tile(running, tile_number):
        grad_keys, grad_values = running
        first_row = tile_number * tile_row_list
        query_tile = lax.dynamic_slice_in_dim(query_heads, first_row, tile_row_list, 0)
        seg_tile = lax.dynamic_slice_in_dim(seg_row, first_row, tile_row_list, 0)
        grad_tile = lax.dynamic_slice_in_dim(grad_heads, first_row, tile_row_list, 0)
        scores = masked_scores(query_tile, key_heads, seg_tile, seg_row, factor)
        weights = jnp.exp(scores - log_sums[tile_number][:, :, None])
        grad_weights = jnp.einsum(
            "qhd,khd->hqk", grad_tile, value_heads, preferred_element_type=jnp.float32
        )
        weighted = jnp.sum(weights * grad_weights, axis=-1, keepdims=True)
        grad_scores = (weights * (grad_weights - weighted)).astype(jnp.bfloat16)
        grad_query = (
            jnp.einsum("hqk,khd->qhd", grad_scores, key_heads, preferred_element_type=jnp.float32)
            * factor
        )
        grad_keys = (
            grad_keys
            + jnp.einsum(
                "hqk,qhd->khd", grad_scores, query_tile, preferred_element_type=jnp.float32
            )
            * factor
        )
        grad_values = grad_values + jnp.einsum(
            "hqk,qhd->khd",
            weights.astype(jnp.bfloat16),
            grad_tile,
            preferred_element_type=jnp.float32,
        )
        return ((grad_keys, grad_values), grad_query)

    zeros_heads = jnp.zeros((length, head_count, head_width), jnp.float32)
    (grad_keys, grad_values), grad_queries = lax.scan(
        one_tile, (zeros_heads, zeros_heads), jnp.arange(length // tile_row_list)
    )
    return (grad_queries.reshape(length, head_count, head_width), grad_keys, grad_values)


def split_heads(value_list, row_count_total):
    return value_list.reshape(row_count_total, PACKED_ROW_LENGTH, -1, HEAD_SIZE)


def local(
    tokens,
    cotangent,
    prompts,
    segments,
    prompt_slot_index,
    norm_gain,
    norm_shift,
    attn_qkv,
    attn_bias,
    attn_out,
    mlp_weight,
    mlp_bias_up,
    mlp_bias_down,
):
    token_tally = tokens.shape[0]
    feature_count = tokens.shape[1]
    row_count_total = token_tally // PACKED_ROW_LENGTH
    tile_row_list = min(512, PACKED_ROW_LENGTH)
    qkv_all, out_all = (
        lax.all_gather(attn_qkv, ("dp", "mp"), axis=1, tiled=True),
        lax.all_gather(attn_out, ("dp", "mp"), axis=0, tiled=True),
    )
    mlp_part = lax.all_gather(mlp_weight, "dp", axis=1, tiled=True)
    input_list = tokens.astype(jnp.float32)
    prompt_table = jnp.concatenate([prompts, jnp.zeros((1, feature_count), jnp.float32)], 0)
    onehot = (
        prompt_slot_index[:, None] == jnp.arange(NPROMPT + 1, dtype=jnp.int32)[None, :]
    ).astype(jnp.float32)
    is_prompt = (prompt_slot_index < NPROMPT)[:, None]
    start = jnp.where(is_prompt, jnp.dot(onehot, prompt_table, precision=HIGHEST), input_list)
    normed_one = layer_norm(start, norm_gain[0], norm_shift[0]).astype(jnp.bfloat16)
    projected = jnp.einsum("td,cde->cte", normed_one, qkv_all, preferred_element_type=jnp.float32)
    queries = (projected[0] + attn_bias[0]).astype(jnp.bfloat16)
    key_rows = projected[1].astype(jnp.bfloat16)
    value_rows = (projected[2] + attn_bias[1]).astype(jnp.bfloat16)
    segment_row_list = segments.reshape(row_count_total, PACKED_ROW_LENGTH)
    query_split = split_heads(queries, row_count_total)
    key_split = split_heads(key_rows, row_count_total)
    value_split = split_heads(value_rows, row_count_total)
    mixed, log_sums = lax.map(
        partial(attend_forward, tile_row_list=tile_row_list),
        (query_split, key_split, value_split, segment_row_list),
    )
    mixed = mixed.reshape(token_tally, feature_count)
    middle = start + jnp.dot(mixed, out_all, preferred_element_type=jnp.float32) + attn_bias[2]
    normed_two = layer_norm(middle, norm_gain[1], norm_shift[1]).astype(jnp.bfloat16)
    grad_output = cotangent.astype(jnp.float32)
    grad_down = jnp.sum(grad_output, axis=0)
    gathered = lax.all_gather(normed_two, "mp", axis=0, tiled=True)
    unit_count = mlp_part.shape[2]
    offset = lax.axis_index("mp") * unit_count
    bias_part = lax.dynamic_slice_in_dim(mlp_bias_up, offset, unit_count, 0)
    before = jnp.dot(gathered, mlp_part[0], preferred_element_type=jnp.float32) + bias_part
    hidden = gelu_exact(before).astype(jnp.bfloat16)
    piece = hidden
    branch = lax.psum_scatter(
        jnp.einsum("tf,df->td", piece, mlp_part[1], preferred_element_type=jnp.float32).astype(
            jnp.bfloat16
        ),
        "mp",
        scatter_dimension=0,
        tiled=True,
    ).astype(jnp.float32)
    output = middle + branch + mlp_bias_down
    grad_gathered = lax.all_gather(cotangent, "mp", axis=0, tiled=True)
    grad_hidden = jnp.dot(grad_gathered, mlp_part[1], preferred_element_type=jnp.float32)
    before_out, gelu_pull = jax.vjp(gelu_exact, before)
    grad_before = gelu_pull(grad_hidden)[0].astype(jnp.bfloat16)
    grad_mlp = jnp.stack(
        [
            jnp.einsum("td,tf->df", gathered, grad_before, preferred_element_type=jnp.float32),
            jnp.einsum("td,tf->df", grad_gathered, hidden, preferred_element_type=jnp.float32),
        ]
    )
    grad_up = lax.dynamic_update_slice_in_dim(
        jnp.zeros_like(mlp_bias_up), jnp.sum(grad_before.astype(jnp.float32), axis=0), offset, 0
    )
    piece = grad_before
    grad_normed_two = lax.psum_scatter(
        jnp.einsum("tf,df->td", piece, mlp_part[0], preferred_element_type=jnp.float32).astype(
            jnp.bfloat16
        ),
        "mp",
        scatter_dimension=0,
        tiled=True,
    ).astype(jnp.float32)
    mlp_grad = lax.psum_scatter(grad_mlp, "dp", scatter_dimension=1, tiled=True)
    norm_out_two, pull_two = jax.vjp(layer_norm, middle, norm_gain[1], norm_shift[1])
    grad_from_two, grad_gain_two, grad_shift_two = pull_two(grad_normed_two)
    grad_middle = grad_output + grad_from_two
    grad_branch = grad_middle.astype(jnp.bfloat16)
    grad_bias_out = jnp.sum(grad_branch.astype(jnp.float32), axis=0)
    grad_out_weight = jnp.einsum(
        "td,te->de", mixed, grad_branch, preferred_element_type=jnp.float32
    )
    grad_mixed = jnp.einsum(
        "te,de->td", grad_branch, out_all, preferred_element_type=jnp.float32
    ).astype(jnp.bfloat16)
    grad_queries, grad_keys, grad_values = lax.map(
        partial(attend_backward, tile_row_list=tile_row_list),
        (
            query_split,
            key_split,
            value_split,
            segment_row_list,
            log_sums,
            split_heads(grad_mixed, row_count_total),
        ),
    )
    grad_projected = jnp.stack(
        [
            grad_queries.reshape(token_tally, feature_count),
            grad_keys.reshape(token_tally, feature_count),
            grad_values.reshape(token_tally, feature_count),
        ]
    ).astype(jnp.bfloat16)
    grad_qkv = jnp.einsum(
        "td,cte->cde", normed_one, grad_projected, preferred_element_type=jnp.float32
    )
    grad_attn_bias = jnp.stack(
        [
            jnp.sum(grad_projected[0].astype(jnp.float32), axis=0),
            jnp.sum(grad_projected[2].astype(jnp.float32), axis=0),
            grad_bias_out,
        ]
    )
    grad_normed_one = jnp.einsum(
        "cte,cde->td", grad_projected, qkv_all, preferred_element_type=jnp.float32
    )
    norm_out_one, pull_one = jax.vjp(layer_norm, start, norm_gain[0], norm_shift[0])
    grad_from_one, grad_gain_one, grad_shift_one = pull_one(grad_normed_one)
    grad_start = grad_middle + grad_from_one
    input_grad = jnp.where(is_prompt, 0.0, grad_start)
    grad_prompts = jnp.dot(onehot.T, grad_start, precision=HIGHEST)[:NPROMPT]
    qkv_grad, out_grad = (
        lax.psum_scatter(grad_qkv, ("dp", "mp"), scatter_dimension=1, tiled=True),
        lax.psum_scatter(grad_out_weight, ("dp", "mp"), scatter_dimension=0, tiled=True),
    )
    summed = lax.psum(
        (
            grad_prompts,
            jnp.stack([grad_gain_one, grad_gain_two]),
            jnp.stack([grad_shift_one, grad_shift_two]),
            grad_attn_bias,
            grad_up,
            grad_down,
        ),
        ("dp", "mp"),
    )
    return (
        output.astype(jnp.bfloat16),
        input_grad,
        summed[0],
        summed[1],
        summed[2],
        qkv_grad,
        summed[3],
        out_grad,
        mlp_grad,
        summed[4],
        summed[5],
    )


def solution(mesh):
    return jax.shard_map(
        local,
        mesh=mesh,
        in_specs=(
            P(("dp", "mp"), None),
            P(("dp", "mp"), None),
            P(),
            P(("dp", "mp")),
            P(("dp", "mp")),
            P(),
            P(),
            P(None, ("dp", "mp"), None),
            P(),
            P(("dp", "mp"), None),
            P(None, "dp", "mp"),
            P(),
            P(),
        ),
        out_specs=(
            P(("dp", "mp"), None),
            P(("dp", "mp"), None),
            P(),
            P(),
            P(),
            P(None, ("dp", "mp"), None),
            P(),
            P(("dp", "mp"), None),
            P(None, "dp", "mp"),
            P(),
            P(),
        ),
        check_vma=False,
    )
```

profile of v0, /device:TPU:0, one launch (start us, length us, event | category | flops | bytes accessed | tf_op | source)
XLA Modules:
  0.0 1018.5 jit_solution(4451620781767088363)
XLA Ops:
  21.6 52.1 %all-gather.6.cloned.1.call-done = bf16[3,768,768]{2,1,0:T(8,128)(2,1)} async-done(((bf16[3,24,768]{2,1,0:T(8,128)(2,1)}), bf16[3,768,768]{2,1,0:T(8,128)(2,1)}) %all-gather.6.cloned.1.call-update) | async-done | bytes 3538960 | tf_op jit(solution)/shard_map/all_gather | solution.py:122
  73.7 6.2 convolution_bitcast_fusion
  82.9 73.5 %while.47 = (s32[]{:T(128)}, bf16[2,512,12,64]{1,3,2,0:T(8,128)(2,1)}, f32[2,12,512]{2,1,0:T(8,128)S(1)}, s32[2]{0:T(128)S(1)}, s32[1024]{0:T(1024)S(1)}, /*inde...) while((s32[]{:T(128)}, ...), condition=%wide.region_5.6_spmd, body=%wide.region_2.5_spmd.sunk | while | flops 1687021568 | bytes 189499632 | solution.py:51
  85.1 10.6 %fusion.103 = (f32[12,512]{1,0:T(8,128)S(1)}, f32[12,512,1024]{2,1,0:T(8,128)}) fusion(pred[512,1024]{1,0:T(8,128)(4,1)S(1)} %broadcast_compare_fusion.5, bf16[1024,12,64]{0,2,1:T(8,128)(2,1)S(1)} %get-tuple-element.478, bf16[1024,12,64]{0,2,1:T(8,128)(2,1)S(1)} %get-tuple-element.477, s32[]{:T(128)S(6)} %select_n.77), kind=kOutput, calls=%fused_computation.3.clone.1 | convolution fusion | flops 824174592 | bytes 28073988 | tf_op jit(solution)/shard_map/while/body/eval_jaxpr/while/body/eval_jaxpr/qhd,khd->hqk/dot_general | solution.py:28
  95.7 12.3 %fusion.104 = f32[12,512]{1,0:T(8,128)S(1)} fusion(f32[12,512,1024]{2,1,0:T(8,128)} %get-tuple-element.433, f32[12,512]{1,0:T(8,128)S(1)} %get-tuple-element.434, pred[512,1024]{1,0:T(8,128)(4,1)S(1)} %broadcast_compare_fusion.5), kind=kLoop, calls=%fused_computation.4.clone.1 | loop fusion | flops 25159680 | bytes 25739264 | tf_op jit(solution)/shard_map/while/body/eval_jaxpr/while/body/eval_jaxpr/reduce_sum | solution.py:46
  111.2 8.5 fusion.105
  121.4 10.7 %fusion.103 = (f32[12,512]{1,0:T(8,128)S(1)}, f32[12,512,1024]{2,1,0:T(8,128)}) fusion(pred[512,1024]{1,0:T(8,128)(4,1)S(1)} %broadcast_compare_fusion.5, bf16[1024,12,64]{0,2,1:T(8,128)(2,1)S(1)} %get-tuple-element.478, bf16[1024,12,64]{0,2,1:T(8,128)(2,1)S(1)} %get-tuple-element.477, s32[]{:T(128)S(6)} %select_n.77), kind=kOutput, calls=%fused_computation.3.clone.1 | convolution fusion | flops 824174592 | bytes 28073988 | tf_op jit(solution)/shard_map/while/body/eval_jaxpr/while/body/eval_jaxpr/qhd,khd->hqk/dot_general | solution.py:28
  132.1 12.4 %fusion.104 = f32[12,512]{1,0:T(8,128)S(1)} fusion(f32[12,512,1024]{2,1,0:T(8,128)} %get-tuple-element.433, f32[12,512]{1,0:T(8,128)S(1)} %get-tuple-element.434, pred[512,1024]{1,0:T(8,128)(4,1)S(1)} %broadcast_compare_fusion.5), kind=kLoop, calls=%fused_computation.4.clone.1 | loop fusion | flops 25159680 | bytes 25739264 | tf_op jit(solution)/shard_map/while/body/eval_jaxpr/while/body/eval_jaxpr/reduce_sum | solution.py:46
  147.8 8.5 fusion.105
  156.4 4.2 copy.60
  162.3 4.4 fusion.60
  171.4 10.8 %all-gather.12.cloned.1.call-done = bf16[2,768,768]{2,1,0:T(8,128)(2,1)} async-done(((bf16[2,96,768]{2,1,0:T(8,128)(2,1)}), bf16[2,768,768]{2,1,0:T(8,128)(2,1)}) %all-gather.12.cloned.1.call-update) | async-done | bytes 2359312 | tf_op jit(solution)/shard_map/all_gather | solution.py:125
  182.2 46.9 %all-gather.10.cloned.1.call-done = bf16[4096,768]{0,1:T(8,128)(2,1)} async-done(((bf16[1024,768]{0,1:T(8,128)(2,1)}), bf16[4096,768]{0,1:T(8,128)(2,1)}) %all-gather.10.cloned.1.call-update) | async-done | bytes 6291472 | tf_op jit(solution)/shard_map/all_gather | solution.py:151
  229.1 35.4 %multiply_convert_fusion.1 = (bf16[4096,768]{1,0:T(8,128)(2,1)}, f32[4096,768]{1,0:T(8,128)}, f32[4096,768]{1,0:T(8,128)}) fusion(f32[768]{0:T(1024)S(1)} %dynamic_slice.51, bf16[4096,768]{0,1:T(8,128)(2,1)} %all-gather.10.cloned.1.call-done, bf16[2,768,768]{2,1,0:T(8,128)(2,1)} %all-gather.12.cloned.1.call-done), kind=kOutput, calls=%fused_computation.43 | convolution fusion | flops 5039456256 | bytes 38931456 | tf_op jit(solution)/shard_map/dot_general | solution.py:155
  264.5 12.4 %all-gather.14.cloned.1.call-done = bf16[4096,768]{1,0:T(8,128)(2,1)} async-done(((bf16[1024,768]{1,0:T(8,128)(2,1)}), bf16[4096,768]{1,0:T(8,128)(2,1)}) %all-gather.14.cloned.1.call-update) | async-done | bytes 6291472 | tf_op jit(solution)/shard_map/all_gather | solution.py:167
  276.9 15.2 %convert_reduce_fusion = (f32[768]{0:T(1024)}, bf16[4096,768]{1,0:T(8,128)(2,1)S(1)}) fusion(f32[4096,768]{1,0:T(8,128)} %get-tuple-element.303, bf16[4096,768]{1,0:T(8,128)(2,1)} %all-gather.14.cloned.1.call-done, bf16[2,768,768]{2,1,0:T(8,128)(2,1)S(1)} %copy-done.65, f32[4096,768]{1,0:T(8,128)} %get-tuple-element.317, f32[768]{0:T(1024)S(1)} %dynamic_slice.51), kind=kOutput, calls=%fused_computation.41 | convolution fusion | flops 4885314560 | bytes 38935552 | tf_op jit(solution)/shard_map/dot_general | solution.py:168
  294.7 6.9 convolution_convert_fusion
  305.6 9.9 convolution_convert_fusion.1
  315.6 44.2 %reduce-scatter.7.cloned.1.call-done = bf16[1024,768]{0,1:T(8,128)(2,1)} async-done(((bf16[4096,768]{0,1:T(8,128)(2,1)}), bf16[1024,768]{0,1:T(8,128)(2,1)}) %reduce-scatter.7.cloned.1.call-update) | async-done | bytes 1572880 | tf_op jit(solution)/shard_map/reduce_scatter | solution.py:181
  369.8 175.1 %while.48 = (s32[]{:T(128)}, f32[1024,12,64]{0,2,1:T(8,128)}, f32[1024,12,64]{0,2,1:T(8,128)}, bf16[2,512,12,64]{1,3,2,0:T(8,128)(2,1)}, s32[2]{0:T(128)S(1)}, /...) while((s32[]{:T(128)}, f32[1024,12,64]{0,2,1:T(8,128)}, ...), condition=%wide.region_14.15_spmd.clone, body=%wide.region_12.14_spmd.clone.sunk | while | flops 4125747200 | bytes 225634640 | solution.py:92
  373.9 12.1 %fusion.115 = f32[12,512,1024]{2,1,0:T(8,128)} fusion(bf16[1024,12,64]{0,2,1:T(8,128)(2,1)S(1)} %get-tuple-element.523, bf16[1024,12,64]{0,2,1:T(8,128)(2,1)} %get-tuple-element.521, s32[]{:T(128)S(6)} %select_n.81), kind=kOutput, calls=%fused_computation.30.clone.1 | convolution fusion | flops 805306368 | bytes 27525124 | tf_op jit(solution)/shard_map/while/body/eval_jaxpr/while/body/eval_jaxpr/qhd,khd->hqk/dot_general | solution.py:28
  386.1 13.3 %bitcast_add_fusion.5 = f32[1024,12,64]{0,2,1:T(8,128)} fusion(f32[1024,12,64]{0,2,1:T(8,128)} %get-tuple-element.502, f32[12,512,1024]{2,1,0:T(8,128)} %fusion.115, f32[12,512]{1,0:T(8,128)S(1)} %dynamic-slice_bitcast_fusion.2, pred[512,1024]{1,0:T(8,128)(4,1)S(1)} %broadcast_compare_fusion.6, pred[]{:T(512)S(6)} %compare.4, ...), kind=kOutput, calls=%fused_computation.22.clone.1 | convolution fusion | flops 832045056 | bytes 32800772 | tf_op jit(solution)/shard_map/while/body/eval_jaxpr/while/body/eval_jaxpr/hqk,qhd->khd/dot_general | solution.py:83
  399.4 18.3 %multiply_reduce_fusion.6 = (f32[12,512]{1,0:T(8,128)S(1)}, f32[12,512,1024]{2,1,0:T(8,128)}) fusion(f32[12,512,1024]{2,1,0:T(8,128)} %fusion.115, f32[12,512]{1,0:T(8,128)S(1)} %dynamic-slice_bitcast_fusion.2, pred[512,1024]{1,0:T(8,128)(4,1)S(1)} %broadcast_compare_fusion.6, bf16[1024,12,64]{0,2,1:T(8,128)(2,1)} %get-tuple-element.526, ...), kind=kOutput, calls=%fused_computation.17.clone.1 | convolution fusion | flops 836757504 | bytes 53264388 | tf_op jit(solution)/shard_map/while/body/eval_jaxpr/while/body/eval_jaxpr/qhd,khd->hqk/dot_general | solution.py:67
  417.7 21.4 %multiply_convert_fusion.3 = bf16[12,512,1024]{2,1,0:T(8,128)(2,1)} fusion(f32[12,512,1024]{2,1,0:T(8,128)} %get-tuple-element.446, f32[12,512,1024]{2,1,0:T(8,128)} %fusion.115, f32[12,512]{1,0:T(8,128)S(1)} %get-tuple-element.447, f32[12,512]{1,0:T(8,128)S(1)} %dynamic-slice_bitcast_fusion.2, pred[512,1024]{1,0:T(8,128)(4,1)S(1)} %broadcast_compare_fusion.6), kind=kLoop, calls=%fused_computation.16.clone.1 | loop fusion | flops 37748736 | bytes 63488000 | tf_op jit(solution)/shard_map/while/body/eval_jaxpr/while/body/eval_jaxpr/convert_element_type | solution.py:71
  439.0 9.5 bitcast_dynamic-update-slice_fusion.5
  448.5 8.6 bitcast_add_fusion.4
  460.7 11.5 %fusion.115 = f32[12,512,1024]{2,1,0:T(8,128)} fusion(bf16[1024,12,64]{0,2,1:T(8,128)(2,1)S(1)} %get-tuple-element.523, bf16[1024,12,64]{0,2,1:T(8,128)(2,1)} %get-tuple-element.521, s32[]{:T(128)S(6)} %select_n.81), kind=kOutput, calls=%fused_computation.30.clone.1 | convolution fusion | flops 805306368 | bytes 27525124 | tf_op jit(solution)/shard_map/while/body/eval_jaxpr/while/body/eval_jaxpr/qhd,khd->hqk/dot_general | solution.py:28
  472.2 14.2 %bitcast_add_fusion.5 = f32[1024,12,64]{0,2,1:T(8,128)} fusion(f32[1024,12,64]{0,2,1:T(8,128)} %get-tuple-element.502, f32[12,512,1024]{2,1,0:T(8,128)} %fusion.115, f32[12,512]{1,0:T(8,128)S(1)} %dynamic-slice_bitcast_fusion.2, pred[512,1024]{1,0:T(8,128)(4,1)S(1)} %broadcast_compare_fusion.6, pred[]{:T(512)S(6)} %compare.4, ...), kind=kOutput, calls=%fused_computation.22.clone.1 | convolution fusion | flops 832045056 | bytes 32800772 | tf_op jit(solution)/shard_map/while/body/eval_jaxpr/while/body/eval_jaxpr/hqk,qhd->khd/dot_general | solution.py:83
  486.4 18.1 %multiply_reduce_fusion.6 = (f32[12,512]{1,0:T(8,128)S(1)}, f32[12,512,1024]{2,1,0:T(8,128)}) fusion(f32[12,512,1024]{2,1,0:T(8,128)} %fusion.115, f32[12,512]{1,0:T(8,128)S(1)} %dynamic-slice_bitcast_fusion.2, pred[512,1024]{1,0:T(8,128)(4,1)S(1)} %broadcast_compare_fusion.6, bf16[1024,12,64]{0,2,1:T(8,128)(2,1)} %get-tuple-element.526, ...), kind=kOutput, calls=%fused_computation.17.clone.1 | convolution fusion | flops 836757504 | bytes 53264388 | tf_op jit(solution)/shard_map/while/body/eval_jaxpr/while/body/eval_jaxpr/qhd,khd->hqk/dot_general | solution.py:67
  504.5 21.2 %multiply_convert_fusion.3 = bf16[12,512,1024]{2,1,0:T(8,128)(2,1)} fusion(f32[12,512,1024]{2,1,0:T(8,128)} %get-tuple-element.446, f32[12,512,1024]{2,1,0:T(8,128)} %fusion.115, f32[12,512]{1,0:T(8,128)S(1)} %get-tuple-element.447, f32[12,512]{1,0:T(8,128)S(1)} %dynamic-slice_bitcast_fusion.2, pred[512,1024]{1,0:T(8,128)(4,1)S(1)} %broadcast_compare_fusion.6), kind=kLoop, calls=%fused_computation.16.clone.1 | loop fusion | flops 37748736 | bytes 63488000 | tf_op jit(solution)/shard_map/while/body/eval_jaxpr/while/body/eval_jaxpr/convert_element_type | solution.py:71
  525.8 9.5 bitcast_dynamic-update-slice_fusion.5
  535.3 9.5 bitcast_add_fusion.4
  544.9 4.2 copy.64
  549.1 4.0 stack_reshape.12
  565.7 9.4 convolution_bitcast_fusion.1
  575.1 11.0 %copy.72 = f32[3,768,768]{2,0,1:T(4,128)} copy(f32[3,768,768]{1,2,0:T(8,128)} %convolution_bitcast_fusion.1) | data formatting | bytes 14155776 | tf_op jit(solution)/shard_map/td,cte->cde/transpose | solution.py:219
  586.1 9.0 fusion.61
  595.1 3.9 copy.68
  606.8 3.8 fusion.45
  610.6 9.1 convolution_bitcast_fusion.2
  619.7 9.1 convolution_bitcast_fusion.3
  631.4 4.8 fusion.62
  638.6 5.9 broadcast_select_fusion
  644.6 3.7 copy.75
  649.8 41.1 %all-reduce.2 = (f32[2,768]{1,0:T(2,128)}, f32[2,768]{1,0:T(2,128)}, f32[3,768]{1,0:T(4,128)}, f32[3072]{0:T(1024)}, f32[768]{0:T(1024)}) all-reduce(f32[2,768]{1,0:T(2,128)S(1)} %pad_maximum_fusion.7, f32[2,768]{1,0:T(2,128)S(1)} %pad_maximum_fusion.8, ...), channel_id=1, replica_groups=mesh['dp'=8,'mp'=4] {'dp','mp'}, use_global_device_ids=true, to_apply=%region_20.21 | all-reduce | flops 9216 | bytes 73728 | tf_op jit(solution)/shard_map/psum | solution.py:241
  691.0 114.2 %all-reduce.6.cloned.1.call-done = (f32[50,768]{1,0:T(8,128)}, f32[3,768,768]{2,0,1:T(4,128)}) async-done(((f32[50,768]{1,0:T(8,128)}, f32[3,768,768]{2,0,1:T(4,128)}), (f32[50,768]{1,0:T(8,128)}, f32[3,768,768]{2,0,1:T(4,128)})) %all-reduce.6.cloned.1.call-update) | async-done | bytes 7231504 | tf_op jit(solution)/shard_map/psum | solution.py:241
  806.9 98.0 %reduce-scatter.11.cloned.1.call-done = f32[2,96,768]{2,1,0:T(8,128)} async-done(((f32[2,768,768]{2,1,0:T(8,128)}), f32[2,96,768]{2,1,0:T(8,128)}) %reduce-scatter.11.cloned.1.call-update) | async-done | bytes 589840 | tf_op jit(solution)/shard_map/reduce_scatter | solution.py:189
  904.9 104.9 %reduce-scatter.9.cloned.1.call-done = f32[24,768]{1,0:T(8,128)} async-done(((f32[768,768]{1,0:T(8,128)}), f32[24,768]{1,0:T(8,128)}) %reduce-scatter.9.cloned.1.call-update) | async-done | bytes 73744 | tf_op jit(solution)/shard_map/reduce_scatter | solution.py:239
  (244 shorter events, 80.8 us)
Async XLA Ops:
  7.2 9.9 copy-start.50
  7.2 9.9 copy-start.30
  7.2 66.5 %all-gather.6.cloned.1.call-start = ((), (), s32[]{:S(2)}) async-start(), calls=%async_computation.4 | async-start | bytes 3649536 | tf_op jit(solution)/shard_map/all_gather | solution.py:122
  7.9 154.3 %all-gather.8.cloned.1.call-start = ((), (), s32[]{:S(2)}) async-start(), calls=%async_computation.5 | async-start | bytes 1216512 | tf_op jit(solution)/shard_map/all_gather | solution.py:123
  8.7 173.5 %all-gather.12.cloned.1.call-start = ((), (), s32[]{:S(2)}) async-start(), calls=%async_computation.7 | async-start | bytes 2654208 | tf_op jit(solution)/shard_map/all_gather | solution.py:125
  9.4 219.7 %all-gather.10.cloned.1.call-start = ((), (), s32[]{:S(2)}) async-start(), calls=%async_computation.6 | async-start | bytes 7864320 | tf_op jit(solution)/shard_map/all_gather | solution.py:151
  10.2 10.1 copy-start.58
  11.6 62.2 %copy-start.46 = (f32[768]{0:T(1024)}, f32[768]{0:T(1024)S(1)}, u32[]{:S(2)}) copy-start(f32[768]{0:T(1024)S(1)} %get-tuple-element.248) | copy-start | bytes 9220
  12.9 60.8 %copy-start.60 = (f32[768]{0:T(1024)}, f32[768]{0:T(1024)S(1)}, u32[]{:S(2)}) copy-start(f32[768]{0:T(1024)S(1)} %get-tuple-element.250) | copy-start | bytes 9220
  20.3 53.4 %copy-start.10 = (f32[1024,768]{0,1:T(8,128)}, f32[1024,768]{0,1:T(8,128)S(1)}, u32[]{:S(2)}) copy-start(f32[1024,768]{0,1:T(8,128)S(1)} %get-tuple-element.314) | copy-start | bytes 9437188
  20.3 59.6 %copy-start.38 = (f32[1024]{0:T(1024)}, f32[1024]{0:T(1024)S(1)}, u32[]{:S(2)}) copy-start(f32[1024]{0:T(1024)S(1)} %broadcast_multiply_fusion.1) | copy-start | bytes 12292
  21.6 58.3 %copy-start.48 = (f32[1024]{0:T(1024)}, f32[1024]{0:T(1024)S(1)}, u32[]{:S(2)}) copy-start(f32[1024]{0:T(1024)S(1)} %fusion.47) | copy-start | bytes 12292
  85.1 23.0 %copy-start.9 = (bf16[1024,12,64]{0,2,1:T(8,128)(2,1)S(1)}, bf16[1024,12,64]{0,2,1:T(8,128)(2,1)}, u32[]{:S(2)}) copy-start(bf16[1024,12,64]{0,2,1:T(8,128)(2,1)} %get-tuple-element.479) | copy-start | bytes 4718596 | tf_op jit(solution)/shard_map/while/body/eval_jaxpr/while
  95.7 15.4 %copy-start = (f32[12,512,1024]{2,1,0:T(8,128)S(1)}, f32[12,512,1024]{2,1,0:T(8,128)}, u32[]{:S(2)}) copy-start(f32[12,512,1024]{2,1,0:T(8,128)} %get-tuple-element.433) | copy-start | bytes 75497472 | tf_op jit(solution)/shard_map/while/body/eval_jaxpr/while
  121.4 23.1 %copy-start.9 = (bf16[1024,12,64]{0,2,1:T(8,128)(2,1)S(1)}, bf16[1024,12,64]{0,2,1:T(8,128)(2,1)}, u32[]{:S(2)}) copy-start(bf16[1024,12,64]{0,2,1:T(8,128)(2,1)} %get-tuple-element.479) | copy-start | bytes 4718596 | tf_op jit(solution)/shard_map/while/body/eval_jaxpr/while
  132.1 15.7 %copy-start = (f32[12,512,1024]{2,1,0:T(8,128)S(1)}, f32[12,512,1024]{2,1,0:T(8,128)}, u32[]{:S(2)}) copy-start(f32[12,512,1024]{2,1,0:T(8,128)} %get-tuple-element.433) | copy-start | bytes 75497472 | tf_op jit(solution)/shard_map/while/body/eval_jaxpr/while
  156.3 5.9 copy-start.1
  156.3 5.9 copy-start.4
  156.4 5.9 copy-start.25
  156.4 5.9 copy-start.63
  169.9 107.0 %all-gather.14.cloned.1.call-start = ((), (), s32[]{:S(2)}) async-start(), calls=%async_computation.9 | async-start | bytes 7864320 | tf_op jit(solution)/shard_map/all_gather | solution.py:167
  170.5 189.2 %reduce-scatter.7.cloned.1.call-start = ((), (), s32[]{:S(2)}) async-start(), calls=%async_computation.10 | async-start | bytes 7864320 | tf_op jit(solution)/shard_map/reduce_scatter | solution.py:181
  182.2 94.7 %copy-start.65 = (bf16[2,768,768]{2,1,0:T(8,128)(2,1)S(1)}, bf16[2,768,768]{2,1,0:T(8,128)(2,1)}, u32[]{:S(2)}) copy-start(bf16[2,768,768]{2,1,0:T(8,128)(2,1)} %all-gather.12.cloned.1.call-done) | copy-start | bytes 7077892
  301.7 336.9 %reduce-scatter.5.cloned.1.call-start = ((), (), s32[]{:S(2)}) async-start(), calls=%async_computation.8 | async-start | bytes 7864320 | tf_op jit(solution)/shard_map/reduce_scatter | solution.py:158
  315.5 44.3 %copy-start.7 = (f32[1024,768]{0,1:T(8,128)S(1)}, f32[1024,768]{0,1:T(8,128)}, u32[]{:S(2)}) copy-start(f32[1024,768]{0,1:T(8,128)} %copy-done.6) | copy-start | bytes 9437188
  315.5 44.3 %copy-start.28 = (f32[1024]{0:T(1024)S(1)}, f32[1024]{0:T(1024)}, u32[]{:S(2)}) copy-start(f32[1024]{0:T(1024)} %copy-done.27) | copy-start | bytes 12292
  315.5 44.3 %copy-start.32 = (f32[768]{0:T(1024)S(1)}, f32[768]{0:T(1024)}, u32[]{:S(2)}) copy-start(f32[768]{0:T(1024)} %get-tuple-element.247) | copy-start | bytes 9220
  315.5 47.4 %copy-start.45 = (f32[1024]{0:T(1024)S(1)}, f32[1024]{0:T(1024)}, u32[]{:S(2)}) copy-start(f32[1024]{0:T(1024)} %copy-done.44) | copy-start | bytes 12292
  315.5 47.4 %copy-start.36 = (f32[1024]{0:T(1024)S(1)}, f32[1024]{0:T(1024)}, u32[]{:S(2)}) copy-start(f32[1024]{0:T(1024)} %copy-done.35) | copy-start | bytes 12292
  315.5 489.6 %all-reduce.6.cloned.1.call-start = ((), (), s32[]{:S(2)}) async-start(), calls=%async_computation.13 | async-start | bytes 19218432 | tf_op jit(solution)/shard_map/psum | solution.py:241
  362.9 4.3 copy-start.40
  373.9 12.2 %copy-start.19 = (bf16[1024,12,64]{0,2,1:T(8,128)(2,1)S(1)}, bf16[1024,12,64]{0,2,1:T(8,128)(2,1)}, u32[]{:S(2)}) copy-start(bf16[1024,12,64]{0,2,1:T(8,128)(2,1)} %get-tuple-element.525) | copy-start | bytes 4718596 | tf_op jit(solution)/shard_map/while/body/eval_jaxpr/while
  439.0 9.5 copy-start.5
  460.7 11.5 %copy-start.19 = (bf16[1024,12,64]{0,2,1:T(8,128)(2,1)S(1)}, bf16[1024,12,64]{0,2,1:T(8,128)(2,1)}, u32[]{:S(2)}) copy-start(bf16[1024,12,64]{0,2,1:T(8,128)(2,1)} %get-tuple-element.525) | copy-start | bytes 4718596 | tf_op jit(solution)/shard_map/while/body/eval_jaxpr/while
  525.8 9.5 copy-start.5
  549.1 6.6 copy-start.3
  559.7 6.0 copy-start.11
  559.7 6.0 copy-start.39
  559.7 6.0 copy-start.47
  559.7 6.0 copy-start.49
  559.7 6.0 copy-start.61
  602.8 4.0 copy-start.29
  610.6 294.3 %reduce-scatter.11.cloned.1.call-start = ((), (), s32[]{:S(2)}) async-start(), calls=%async_computation.12 | async-start | bytes 5308416 | tf_op jit(solution)/shard_map/reduce_scatter | solution.py:189
  631.3 4.9 copy-start.62
  631.4 5.5 copy-start.55
  631.4 5.5 copy-start.56
  631.4 5.5 copy-start.57
  631.4 378.4 %reduce-scatter.9.cloned.1.call-start = ((), (), s32[]{:S(2)}) async-start(), calls=%async_computation.11 | async-start | bytes 2433024 | tf_op jit(solution)/shard_map/reduce_scatter | solution.py:239
  (34 other events, 86.7 us)
Sparse Core Ops, SparseCore 0:
  10.9 62.7 all-gather.5
  76.6 52.6 all-gather.7
  131.6 50.5 all-gather.11
  184.2 44.8 all-gather.9
  230.5 46.3 all-gather.13
  301.8 57.8 reduce-scatter.6
  362.3 57.8 reduce-scatter.4
  610.7 194.4 all-reduce.5
  809.4 95.4 reduce-scatter.10
  910.6 99.1 reduce-scatter.8
where the time goes:
time: 1030 us; the launch traced here: 1020 us
  waiting for transfers between devices  486 us (47%)
  matrix products  292 us (28%)
  other arithmetic  100 us (10%)
  local copies, waits for them, and re-layouts  75.8 us (7%)
  blocking collectives  41.1 us (4%)
  between operations  15.2 us (1%)
    psum x1, waiting for transfers between devices, local(): lax.psum((grad_prompts, jnp.stack([grad_gain_one, grad_gain_two]), jnp.st...  114 us
    reduce_scatter x1, waiting for transfers between devices, local(): lax.psum_scatter(grad_out_weight, ('dp', 'mp'), scatter_dimension=0, tile...  105 us
    reduce_scatter x1, waiting for transfers between devices, local(): mlp_grad = lax.psum_scatter(grad_mlp, 'dp', scatter_dimension=1, tiled=True)  98 us
    all_gather x1, waiting for transfers between devices, local(): lax.all_gather(attn_qkv, ('dp', 'mp'), axis=1, tiled=True)  52.1 us
    all_gather x1, waiting for transfers between devices, local(): gathered = lax.all_gather(normed_two, 'mp', axis=0, tiled=True)  46.9 us
    dot_general x4, matrix products, masked_scores(): jnp.einsum('qhd,khd->hqk', query_tile, key_heads, preferred_element_type=...  44.9 us
    reduce_scatter x1, waiting for transfers between devices, local(): lax.psum_scatter(jnp.einsum('tf,df->td', piece, mlp_part[0], preferred_el...  44.2 us
    convert_element_type x2, other arithmetic, one_tile(): grad_scores = (weights * (grad_weights - weighted)).astype(jnp.bfloat16)  42.6 us
  transfers between devices with their start and end apart: 10, of which 8 were waited for; matrix products, arithmetic and copies ran while one was open for 42% of the time, Pallas kernels for 0%

commit v1 on v0

--- a/solution.py
+++ b/solution.py
@@ -10,6 +10,12 @@
 EPS = 1e-06
 HIGHEST = lax.Precision.HIGHEST
 MASKED = -1e30
+
+
+def joined_along(blocks, dim):
+    blocks = jnp.moveaxis(blocks, 0, dim)
+    shape = blocks.shape
+    return blocks.reshape(*shape[:dim], shape[dim] * shape[dim + 1], *shape[dim + 2 :])
 
 
 def layer_norm(value_list, gain_row, shift_row):
@@ -148,7 +154,14 @@
     normed_two = layer_norm(middle, norm_gain[1], norm_shift[1]).astype(jnp.bfloat16)
     grad_output = cotangent.astype(jnp.float32)
     grad_down = jnp.sum(grad_output, axis=0)
-    gathered = lax.all_gather(normed_two, "mp", axis=0, tiled=True)
+    devices = lax.axis_size("mp")
+    right = [(i, (i + 1) % devices) for i in range(devices)]
+    pieces = [normed_two]
+    while len(pieces) < devices:
+        pieces.append(lax.ppermute(pieces[-1], "mp", right))
+    index = lax.axis_index("mp")
+    pieces = jnp.stack(pieces)[(index - jnp.arange(devices)) % devices]
+    gathered = joined_along(pieces, 0)
     unit_count = mlp_part.shape[2]
     offset = lax.axis_index("mp") * unit_count
     bias_part = lax.dynamic_slice_in_dim(mlp_bias_up, offset, unit_count, 0)

time: 1030 us -> 906 us (0.88)
  waiting for transfers between devices: 486 us -> 342 us
  local copies, waits for them, and re-layouts: 75.8 us -> 89.9 us
    reduce_scatter x1, waiting for transfers between devices: 98 us -> 0.01 us  [local(): mlp_grad = lax.psum_scatter(grad_mlp, 'dp', scatter_dimension=1, tiled=True)]
    reduce_scatter x1, waiting for transfers between devices: 105 us -> 31.4 us  [local(): lax.psum_scatter(grad_out_weight, ('dp', 'mp'), scatter_dimension=0, tile...]
    ppermute x0 -> x3, waiting for transfers between devices: none -> 58.8 us  [local(): pieces.append(lax.ppermute(pieces[-1], 'mp', right))]
    all_gather x1 -> x0, waiting for transfers between devices: 46.9 us -> none  [local(): gathered = lax.all_gather(normed_two, 'mp', axis=0, tiled=True)]
    psum x1, waiting for transfers between devices: 114 us -> 155 us  [local(): lax.psum((grad_prompts, jnp.stack([grad_gain_one, grad_gain_two]), jnp.st...]
    gather x0 -> x2, local copies, waits for them, and re-layouts: none -> 15.1 us  [local(): pieces = jnp.stack(pieces)[(index - jnp.arange(devices)) % devices]]
    all_gather x1, waiting for transfers between devices: 12.4 us -> 0.01 us  [local(): grad_gathered = lax.all_gather(cotangent, 'mp', axis=0, tiled=True)]
    all_gather x1, waiting for transfers between devices: 10.8 us -> 0.01 us  [local(): mlp_part = lax.all_gather(mlp_weight, 'dp', axis=1, tiled=True)]
  transfers between devices with their start and end apart: 10 -> 12, of which waited for: 8 -> 7; matrix products, arithmetic and copies ran while one was open for 42% -> 49% of each run, Pallas kernels for 0% -> 0%
where the time goes in v1:
time: 906 us; the launch traced here: 898 us
  waiting for transfers between devices  342 us (38%)
  matrix products  291 us (32%)
  other arithmetic  107 us (12%)
  local copies, waits for them, and re-layouts  89.9 us (10%)
  blocking collectives  43.2 us (5%)
  between operations  16.3 us (2%)
    psum x1, waiting for transfers between devices, local(): lax.psum((grad_prompts, jnp.stack([grad_gain_one, grad_gain_two]), jnp.st...  155 us
    ppermute x3, waiting for transfers between devices, local(): pieces.append(lax.ppermute(pieces[-1], 'mp', right))  58.8 us
    all_gather x1, waiting for transfers between devices, local(): lax.all_gather(attn_qkv, ('dp', 'mp'), axis=1, tiled=True)  52.8 us
    dot_general x4, matrix products, masked_scores(): jnp.einsum('qhd,khd->hqk', query_tile, key_heads, preferred_element_type=...  45 us
    psum x1, blocking collectives, local(): lax.psum((grad_prompts, jnp.stack([grad_gain_one, grad_gain_two]), jnp.st...  43.2 us
    reduce_scatter x1, waiting for transfers between devices, local(): lax.psum_scatter(jnp.einsum('tf,df->td', piece, mlp_part[0], preferred_el...  42.9 us
    convert_element_type x2, other arithmetic, one_tile(): grad_scores = (weights * (grad_weights - weighted)).astype(jnp.bfloat16)  42.6 us
    dot_general x2, matrix products, one_tile(): jnp.einsum('qhd,khd->hqk', grad_tile, value_heads, preferred_element_type...  36.4 us
  transfers between devices with their start and end apart: 12, of which 7 were waited for; matrix products, arithmetic and copies ran while one was open for 49% of the time, Pallas kernels for 0%

profile of v1, /device:TPU:0, one launch (start us, length us, event | category | flops | bytes accessed | tf_op | source)
XLA Modules:
  0.0 898.0 jit_solution(10787307791852259950)
XLA Ops:
  21.7 52.8 %all-gather.5.cloned.1.call-done = bf16[3,768,768]{2,1,0:T(8,128)(2,1)} async-done(((bf16[3,24,768]{2,1,0:T(8,128)(2,1)}), bf16[3,768,768]{2,1,0:T(8,128)(2,1)}) %all-gather.5.cloned.1.call-update) | async-done | bytes 3538960 | tf_op jit(solution)/shard_map/all_gather | solution.py:128
  74.6 6.2 convolution_bitcast_fusion
  83.7 72.8 %while.47 = (s32[]{:T(128)}, bf16[2,512,12,64]{1,3,2,0:T(8,128)(2,1)}, f32[2,12,512]{2,1,0:T(8,128)S(1)}, s32[2]{0:T(128)S(1)}, s32[1024]{0:T(1024)S(1)}, /*inde...) while((s32[]{:T(128)}, ...), condition=%wide.region_5.6_spmd, body=%wide.region_2.5_spmd.sunk | while | flops 1687021568 | bytes 189499632 | solution.py:57
  85.6 10.6 %fusion.106 = (f32[12,512]{1,0:T(8,128)S(1)}, f32[12,512,1024]{2,1,0:T(8,128)}) fusion(pred[512,1024]{1,0:T(8,128)(4,1)S(1)} %broadcast_compare_fusion.5, bf16[1024,12,64]{0,2,1:T(8,128)(2,1)S(1)} %get-tuple-element.478, bf16[1024,12,64]{0,2,1:T(8,128)(2,1)S(1)} %get-tuple-element.477, s32[]{:T(128)S(6)} %select_n.111), kind=kOutput, calls=%fused_computation.4.clone.1 | convolution fusion | flops 824174592 | bytes 28073988 | tf_op jit(solution)/shard_map/while/body/eval_jaxpr/while/body/eval_jaxpr/qhd,khd->hqk/dot_general | solution.py:34
  96.2 12.3 %fusion.107 = f32[12,512]{1,0:T(8,128)S(1)} fusion(f32[12,512,1024]{2,1,0:T(8,128)} %get-tuple-element.433, f32[12,512]{1,0:T(8,128)S(1)} %get-tuple-element.434, pred[512,1024]{1,0:T(8,128)(4,1)S(1)} %broadcast_compare_fusion.5), kind=kLoop, calls=%fused_computation.5.clone.1 | loop fusion | flops 25159680 | bytes 25739264 | tf_op jit(solution)/shard_map/while/body/eval_jaxpr/while/body/eval_jaxpr/reduce_sum | solution.py:52
  111.6 8.5 fusion.108
  121.9 10.7 %fusion.106 = (f32[12,512]{1,0:T(8,128)S(1)}, f32[12,512,1024]{2,1,0:T(8,128)}) fusion(pred[512,1024]{1,0:T(8,128)(4,1)S(1)} %broadcast_compare_fusion.5, bf16[1024,12,64]{0,2,1:T(8,128)(2,1)S(1)} %get-tuple-element.478, bf16[1024,12,64]{0,2,1:T(8,128)(2,1)S(1)} %get-tuple-element.477, s32[]{:T(128)S(6)} %select_n.111), kind=kOutput, calls=%fused_computation.4.clone.1 | convolution fusion | flops 824174592 | bytes 28073988 | tf_op jit(solution)/shard_map/while/body/eval_jaxpr/while/body/eval_jaxpr/qhd,khd->hqk/dot_general | solution.py:34
  132.6 12.3 %fusion.107 = f32[12,512]{1,0:T(8,128)S(1)} fusion(f32[12,512,1024]{2,1,0:T(8,128)} %get-tuple-element.433, f32[12,512]{1,0:T(8,128)S(1)} %get-tuple-element.434, pred[512,1024]{1,0:T(8,128)(4,1)S(1)} %broadcast_compare_fusion.5), kind=kLoop, calls=%fused_computation.5.clone.1 | loop fusion | flops 25159680 | bytes 25739264 | tf_op jit(solution)/shard_map/while/body/eval_jaxpr/while/body/eval_jaxpr/reduce_sum | solution.py:52
  148.0 8.5 fusion.108
  156.5 4.2 copy.61
  162.4 4.2 fusion.62
  169.6 19.9 %collective-permute-done = bf16[1024,768]{0,1:T(8,128)(2,1)} collective-permute-done((bf16[1024,768]{0,1:T(8,128)(2,1)}, bf16[1024,768]{0,1:T(8,128)(2,1)}, u32[]{:S(2)}, u32[]{:S(2)}) %collective-permute-start) | collective-permute-done | bytes 1572896 | tf_op jit(solution)/shard_map/ppermute | solution.py:161
  189.5 20.2 %collective-permute-done.1 = bf16[1024,768]{0,1:T(8,128)(2,1)} collective-permute-done((bf16[1024,768]{0,1:T(8,128)(2,1)}, bf16[1024,768]{0,1:T(8,128)(2,1)}, u32[]{:S(2)}, u32[]{:S(2)}) %collective-permute-start.1) | collective-permute-done | bytes 1572896 | tf_op jit(solution)/shard_map/ppermute | solution.py:161
  211.0 18.7 %collective-permute-done.2 = bf16[1024,768]{0,1:T(8,128)(2,1)} collective-permute-done((bf16[1024,768]{0,1:T(8,128)(2,1)}, bf16[1024,768]{0,1:T(8,128)(2,1)}, u32[]{:S(2)}, u32[]{:S(2)}) %collective-permute-start.2) | collective-permute-done | bytes 1572896 | tf_op jit(solution)/shard_map/ppermute | solution.py:161
  229.8 6.7 pad_maximum_fusion
  236.4 6.4 gather_fusion
  242.8 8.7 copy.62
  251.6 34.7 %multiply_convert_fusion.1 = (bf16[4096,768]{1,0:T(8,128)(2,1)}, f32[4096,768]{1,0:T(8,128)}, f32[4096,768]{1,0:T(8,128)}) fusion(f32[768]{0:T(1024)S(1)} %dynamic_slice.51, bf16[4096,768]{1,0:T(8,128)(2,1)} %bitcast.130, bf16[2,768,768]{2,1,0:T(8,128)(2,1)} %all-gather.9.cloned.1.call-done), kind=kOutput, calls=%fused_computation.44 | convolution fusion | flops 5039456256 | bytes 38931456 | tf_op jit(solution)/shard_map/dot_general | solution.py:168
  286.3 15.2 %convert_reduce_fusion = (f32[768]{0:T(1024)}, bf16[4096,768]{1,0:T(8,128)(2,1)S(1)}) fusion(f32[4096,768]{1,0:T(8,128)} %get-tuple-element.303, bf16[4096,768]{1,0:T(8,128)(2,1)} %all-gather.11.cloned.1.call-done, bf16[2,768,768]{2,1,0:T(8,128)(2,1)S(1)} %copy-done.65, f32[4096,768]{1,0:T(8,128)} %get-tuple-element.317, f32[768]{0:T(1024)S(1)} %dynamic_slice.51), kind=kOutput, calls=%fused_computation.42 | convolution fusion | flops 4885314560 | bytes 38935552 | tf_op jit(solution)/shard_map/dot_general | solution.py:181
  304.1 7.0 convolution_convert_fusion
  315.0 9.6 %convolution_convert_fusion.1 = bf16[4096,768]{0,1:T(8,128)(2,1)} fusion(bf16[4096,768]{1,0:T(8,128)(2,1)} %get-tuple-element.302, bf16[2,768,768]{2,1,0:T(8,128)(2,1)} %all-gather.9.cloned.1.call-done), kind=kOutput, calls=%fused_computation.59 | convolution fusion | flops 4834983936 | bytes 13762560 | tf_op jit(solution)/shard_map/tf,df->td/dot_general | solution.py:172
  324.7 42.9 %reduce-scatter.7.cloned.1.call-done = bf16[1024,768]{0,1:T(8,128)(2,1)} async-done(((bf16[4096,768]{0,1:T(8,128)(2,1)}), bf16[1024,768]{0,1:T(8,128)(2,1)}) %reduce-scatter.7.cloned.1.call-update) | async-done | bytes 1572880 | tf_op jit(solution)/shard_map/reduce_scatter | solution.py:194
  377.7 175.1 %while.48 = (s32[]{:T(128)}, f32[1024,12,64]{0,2,1:T(8,128)}, f32[1024,12,64]{0,2,1:T(8,128)}, bf16[2,512,12,64]{1,3,2,0:T(8,128)(2,1)}, s32[2]{0:T(128)S(1)}, /...) while((s32[]{:T(128)}, f32[1024,12,64]{0,2,1:T(8,128)}, ...), condition=%wide.region_14.15_spmd.clone, body=%wide.region_12.14_spmd.clone.sunk | while | flops 4125747200 | bytes 225634640 | solution.py:98
  381.5 12.2 %fusion.118 = f32[12,512,1024]{2,1,0:T(8,128)} fusion(bf16[1024,12,64]{0,2,1:T(8,128)(2,1)S(1)} %get-tuple-element.523, bf16[1024,12,64]{0,2,1:T(8,128)(2,1)} %get-tuple-element.521, s32[]{:T(128)S(6)} %select_n.115), kind=kOutput, calls=%fused_computation.31.clone.1 | convolution fusion | flops 805306368 | bytes 27525124 | tf_op jit(solution)/shard_map/while/body/eval_jaxpr/while/body/eval_jaxpr/qhd,khd->hqk/dot_general | solution.py:34
  393.7 13.3 %bitcast_add_fusion.5 = f32[1024,12,64]{0,2,1:T(8,128)} fusion(f32[1024,12,64]{0,2,1:T(8,128)} %get-tuple-element.502, f32[12,512,1024]{2,1,0:T(8,128)} %fusion.118, f32[12,512]{1,0:T(8,128)S(1)} %dynamic-slice_bitcast_fusion.2, pred[512,1024]{1,0:T(8,128)(4,1)S(1)} %broadcast_compare_fusion.6, pred[]{:T(512)S(6)} %compare.11, ...), kind=kOutput, calls=%fused_computation.23.clone.1 | convolution fusion | flops 832045056 | bytes 32800772 | tf_op jit(solution)/shard_map/while/body/eval_jaxpr/while/body/eval_jaxpr/hqk,qhd->khd/dot_general | solution.py:89
  407.0 18.3 %multiply_reduce_fusion.6 = (f32[12,512]{1,0:T(8,128)S(1)}, f32[12,512,1024]{2,1,0:T(8,128)}) fusion(f32[12,512,1024]{2,1,0:T(8,128)} %fusion.118, f32[12,512]{1,0:T(8,128)S(1)} %dynamic-slice_bitcast_fusion.2, pred[512,1024]{1,0:T(8,128)(4,1)S(1)} %broadcast_compare_fusion.6, bf16[1024,12,64]{0,2,1:T(8,128)(2,1)} %get-tuple-element.526, ...), kind=kOutput, calls=%fused_computation.18.clone.1 | convolution fusion | flops 836757504 | bytes 53264388 | tf_op jit(solution)/shard_map/while/body/eval_jaxpr/while/body/eval_jaxpr/qhd,khd->hqk/dot_general | solution.py:73
  425.3 21.4 %multiply_convert_fusion.3 = bf16[12,512,1024]{2,1,0:T(8,128)(2,1)} fusion(f32[12,512,1024]{2,1,0:T(8,128)} %get-tuple-element.446, f32[12,512,1024]{2,1,0:T(8,128)} %fusion.118, f32[12,512]{1,0:T(8,128)S(1)} %get-tuple-element.447, f32[12,512]{1,0:T(8,128)S(1)} %dynamic-slice_bitcast_fusion.2, pred[512,1024]{1,0:T(8,128)(4,1)S(1)} %broadcast_compare_fusion.6), kind=kLoop, calls=%fused_computation.17.clone.1 | loop fusion | flops 37748736 | bytes 63488000 | tf_op jit(solution)/shard_map/while/body/eval_jaxpr/while/body/eval_jaxpr/convert_element_type | solution.py:77
  446.7 9.5 %bitcast_dynamic-update-slice_fusion.5 = bf16[2,512,12,64]{1,3,2,0:T(8,128)(2,1)} fusion(bf16[2,512,12,64]{1,3,2,0:T(8,128)(2,1)} %get-tuple-element.503, s32[]{:T(128)S(6)} %copy.104, bf16[12,512,1024]{2,1,0:T(8,128)(2,1)} %multiply_convert_fusion.3, bf16[1024,12,64]{0,2,1:T(8,128)(2,1)S(1)} %get-tuple-element.523), kind=kOutput, calls=%fused_computation.25.clone.1 | convolution fusion | flops 805699584 | bytes 15728644 | tf_op jit(solution)/shard_map/while/body/eval_jaxpr/while/body/eval_jaxpr/hqk,khd->qhd/dot_general | solution.py:79
  456.2 8.6 bitcast_add_fusion.4
  468.4 11.5 %fusion.118 = f32[12,512,1024]{2,1,0:T(8,128)} fusion(bf16[1024,12,64]{0,2,1:T(8,128)(2,1)S(1)} %get-tuple-element.523, bf16[1024,12,64]{0,2,1:T(8,128)(2,1)} %get-tuple-element.521, s32[]{:T(128)S(6)} %select_n.115), kind=kOutput, calls=%fused_computation.31.clone.1 | convolution fusion | flops 805306368 | bytes 27525124 | tf_op jit(solution)/shard_map/while/body/eval_jaxpr/while/body/eval_jaxpr/qhd,khd->hqk/dot_general | solution.py:34
  479.8 14.2 %bitcast_add_fusion.5 = f32[1024,12,64]{0,2,1:T(8,128)} fusion(f32[1024,12,64]{0,2,1:T(8,128)} %get-tuple-element.502, f32[12,512,1024]{2,1,0:T(8,128)} %fusion.118, f32[12,512]{1,0:T(8,128)S(1)} %dynamic-slice_bitcast_fusion.2, pred[512,1024]{1,0:T(8,128)(4,1)S(1)} %broadcast_compare_fusion.6, pred[]{:T(512)S(6)} %compare.11, ...), kind=kOutput, calls=%fused_computation.23.clone.1 | convolution fusion | flops 832045056 | bytes 32800772 | tf_op jit(solution)/shard_map/while/body/eval_jaxpr/while/body/eval_jaxpr/hqk,qhd->khd/dot_general | solution.py:89
  494.0 18.1 %multiply_reduce_fusion.6 = (f32[12,512]{1,0:T(8,128)S(1)}, f32[12,512,1024]{2,1,0:T(8,128)}) fusion(f32[12,512,1024]{2,1,0:T(8,128)} %fusion.118, f32[12,512]{1,0:T(8,128)S(1)} %dynamic-slice_bitcast_fusion.2, pred[512,1024]{1,0:T(8,128)(4,1)S(1)} %broadcast_compare_fusion.6, bf16[1024,12,64]{0,2,1:T(8,128)(2,1)} %get-tuple-element.526, ...), kind=kOutput, calls=%fused_computation.18.clone.1 | convolution fusion | flops 836757504 | bytes 53264388 | tf_op jit(solution)/shard_map/while/body/eval_jaxpr/while/body/eval_jaxpr/qhd,khd->hqk/dot_general | solution.py:73
  512.2 21.2 %multiply_convert_fusion.3 = bf16[12,512,1024]{2,1,0:T(8,128)(2,1)} fusion(f32[12,512,1024]{2,1,0:T(8,128)} %get-tuple-element.446, f32[12,512,1024]{2,1,0:T(8,128)} %fusion.118, f32[12,512]{1,0:T(8,128)S(1)} %get-tuple-element.447, f32[12,512]{1,0:T(8,128)S(1)} %dynamic-slice_bitcast_fusion.2, pred[512,1024]{1,0:T(8,128)(4,1)S(1)} %broadcast_compare_fusion.6), kind=kLoop, calls=%fused_computation.17.clone.1 | loop fusion | flops 37748736 | bytes 63488000 | tf_op jit(solution)/shard_map/while/body/eval_jaxpr/while/body/eval_jaxpr/convert_element_type | solution.py:77
  533.4 9.5 %bitcast_dynamic-update-slice_fusion.5 = bf16[2,512,12,64]{1,3,2,0:T(8,128)(2,1)} fusion(bf16[2,512,12,64]{1,3,2,0:T(8,128)(2,1)} %get-tuple-element.503, s32[]{:T(128)S(6)} %copy.104, bf16[12,512,1024]{2,1,0:T(8,128)(2,1)} %multiply_convert_fusion.3, bf16[1024,12,64]{0,2,1:T(8,128)(2,1)S(1)} %get-tuple-element.523), kind=kOutput, calls=%fused_computation.25.clone.1 | convolution fusion | flops 805699584 | bytes 15728644 | tf_op jit(solution)/shard_map/while/body/eval_jaxpr/while/body/eval_jaxpr/hqk,khd->qhd/dot_general | solution.py:79
  542.9 9.5 %bitcast_add_fusion.4 = f32[1024,12,64]{0,2,1:T(8,128)} fusion(f32[1024,12,64]{0,2,1:T(8,128)} %get-tuple-element.501, bf16[12,512,1024]{2,1,0:T(8,128)(2,1)} %multiply_convert_fusion.3, pred[]{:T(512)S(6)} %compare.11, bf16[1024,12,64]{0,2,1:T(8,128)(2,1)S(1)} %copy-done.8, s32[]{:T(128)S(6)} %select_n.115), kind=kOutput, calls=%fused_computation.24.clone.1 | convolution fusion | flops 807665664 | bytes 19660804 | tf_op jit(solution)/shard_map/while/body/eval_jaxpr/while/body/eval_jaxpr/hqk,qhd->khd/dot_general | solution.py:84
  552.8 4.2 copy.66
  557.0 4.0 stack_reshape.12
  573.6 9.4 %convolution_bitcast_fusion.1 = f32[3,768,768]{1,2,0:T(8,128)} fusion(bf16[1,1024,768]{2,1,0:T(8,128)(2,1)} %copy.69, bf16[1,1024,768]{2,1,0:T(8,128)(2,1)} %copy.68, bf16[1,1024,768]{2,1,0:T(8,128)(2,1)} %copy.67, f32[1024,768]{0,1:T(8,128)S(1)} %copy-done.11, f32[768]{0:T(1024)S(1)} %copy-done.61, f32[768]{0:T(1024)S(1)} %copy-done.48, ...), kind=kOutput, calls=%fused_computation.91 | convolution fusion | flops 3632529408 | bytes 14956544 | tf_op jit(solution)/shard_map/td,cte->cde/dot_general | solution.py:232
  583.0 11.0 %copy.74 = f32[3,768,768]{2,0,1:T(4,128)} copy(f32[3,768,768]{1,2,0:T(8,128)} %convolution_bitcast_fusion.1) | data formatting | bytes 14155776 | tf_op jit(solution)/shard_map/td,cte->cde/transpose | solution.py:232
  594.0 9.0 fusion.63
  602.9 3.9 copy.70
  618.4 9.3 %convolution_bitcast_fusion.3 = f32[1,768,768]{2,1,0:T(8,128)S(1)} fusion(bf16[4096,768]{1,0:T(8,128)(2,1)} %bitcast.131, bf16[4096,768]{1,0:T(8,128)(2,1)} %copy-done.67), kind=kOutput, calls=%fused_computation.97 | convolution fusion | flops 4831838208 | bytes 14942208 | tf_op jit(solution)/shard_map/td,tf->df/dot_general | solution.py:186
  627.8 9.2 %convolution_bitcast_fusion.2 = f32[1,768,768]{2,1,0:T(8,128)S(1)} fusion(bf16[4096,768]{1,0:T(8,128)(2,1)} %get-tuple-element.302, bf16[4096,768]{1,0:T(8,128)(2,1)} %all-gather.11.cloned.1.call-done), kind=kOutput, calls=%fused_computation.96 | convolution fusion | flops 4831838208 | bytes 14942208 | tf_op jit(solution)/shard_map/td,tf->df/dot_general | solution.py:187
  639.6 4.8 fusion.64
  646.9 5.9 broadcast_select_fusion
  658.1 43.2 %all-reduce.2 = (f32[2,768]{1,0:T(2,128)}, f32[2,768]{1,0:T(2,128)}, f32[3,768]{1,0:T(4,128)}, f32[3072]{0:T(1024)}, f32[768]{0:T(1024)}) all-reduce(f32[2,768]{1,0:T(2,128)S(1)} %pad_maximum_fusion.8, f32[2,768]{1,0:T(2,128)S(1)} %pad_maximum_fusion.9, ...), channel_id=1, replica_groups=mesh['dp'=8,'mp'=4] {'dp','mp'}, use_global_device_ids=true, to_apply=%region_20.21 | all-reduce | flops 9216 | bytes 73728 | tf_op jit(solution)/shard_map/psum | solution.py:254
  701.3 154.5 %all-reduce.6.cloned.1.call-done = (f32[50,768]{1,0:T(8,128)}, f32[3,768,768]{2,0,1:T(4,128)}) async-done(((f32[50,768]{1,0:T(8,128)}, f32[3,768,768]{2,0,1:T(4,128)}), (f32[50,768]{1,0:T(8,128)}, f32[3,768,768]{2,0,1:T(4,128)})) %all-reduce.6.cloned.1.call-update) | async-done | bytes 7231504 | tf_op jit(solution)/shard_map/psum | solution.py:254
  857.6 31.4 %reduce-scatter.9.cloned.1.call-done = f32[24,768]{1,0:T(8,128)} async-done(((f32[768,768]{1,0:T(8,128)}), f32[24,768]{1,0:T(8,128)}) %reduce-scatter.9.cloned.1.call-update) | async-done | bytes 73744 | tf_op jit(solution)/shard_map/reduce_scatter | solution.py:252
  (253 shorter events, 86.9 us)
Async XLA Ops:
  8.0 9.2 %copy-start.51 = (s32[1024]{0:T(1024)S(1)}, s32[1024]{0:T(1024)}, u32[]{:S(2)}) copy-start(s32[1024]{0:T(1024)} %param.21) | copy-start | bytes 12292
  8.0 9.2 %copy-start.33 = (f32[50,768]{1,0:T(8,128)S(1)}, f32[50,768]{1,0:T(8,128)}, u32[]{:S(2)}) copy-start(f32[50,768]{1,0:T(8,128)} %param.19) | copy-start | bytes 460804
  8.0 66.5 %all-gather.5.cloned.1.call-start = ((), (), s32[]{:S(2)}) async-start(), calls=%async_computation.4 | async-start | bytes 3649536 | tf_op jit(solution)/shard_map/all_gather | solution.py:128
  8.8 153.6 %all-gather.7.cloned.1.call-start = ((), (), s32[]{:S(2)}) async-start(), calls=%async_computation.5 | async-start | bytes 1216512 | tf_op jit(solution)/shard_map/all_gather | solution.py:129
  9.5 242.0 %all-gather.9.cloned.1.call-start = ((), (), s32[]{:S(2)}) async-start(), calls=%async_computation.6 | async-start | bytes 2654208 | tf_op jit(solution)/shard_map/all_gather | solution.py:131
  10.3 10.1 %copy-start.58 = (pred[1024]{0:T(1024)(128)(4,1)}, pred[1024]{0:T(1024)(128)(4,1)S(1)}, u32[]{:S(2)}) copy-start(pred[1024]{0:T(1024)(128)(4,1)S(1)} %broadcast_compare_fusion.2) | copy-start | bytes 3076
  11.7 62.9 %copy-start.47 = (f32[768]{0:T(1024)}, f32[768]{0:T(1024)S(1)}, u32[]{:S(2)}) copy-start(f32[768]{0:T(1024)S(1)} %get-tuple-element.248) | copy-start | bytes 9220
  13.0 61.5 %copy-start.60 = (f32[768]{0:T(1024)}, f32[768]{0:T(1024)S(1)}, u32[]{:S(2)}) copy-start(f32[768]{0:T(1024)S(1)} %get-tuple-element.250) | copy-start | bytes 9220
  20.4 54.2 %copy-start.10 = (f32[1024,768]{0,1:T(8,128)}, f32[1024,768]{0,1:T(8,128)S(1)}, u32[]{:S(2)}) copy-start(f32[1024,768]{0,1:T(8,128)S(1)} %get-tuple-element.314) | copy-start | bytes 9437188
  20.4 60.4 %copy-start.38 = (f32[1024]{0:T(1024)}, f32[1024]{0:T(1024)S(1)}, u32[]{:S(2)}) copy-start(f32[1024]{0:T(1024)S(1)} %broadcast_multiply_fusion.1) | copy-start | bytes 12292
  21.7 59.0 %copy-start.49 = (f32[1024]{0:T(1024)}, f32[1024]{0:T(1024)S(1)}, u32[]{:S(2)}) copy-start(f32[1024]{0:T(1024)S(1)} %fusion.47) | copy-start | bytes 12292
  85.6 23.0 %copy-start.9 = (bf16[1024,12,64]{0,2,1:T(8,128)(2,1)S(1)}, bf16[1024,12,64]{0,2,1:T(8,128)(2,1)}, u32[]{:S(2)}) copy-start(bf16[1024,12,64]{0,2,1:T(8,128)(2,1)} %get-tuple-element.479) | copy-start | bytes 4718596 | tf_op jit(solution)/shard_map/while/body/eval_jaxpr/while
  96.2 15.4 %copy-start = (f32[12,512,1024]{2,1,0:T(8,128)S(1)}, f32[12,512,1024]{2,1,0:T(8,128)}, u32[]{:S(2)}) copy-start(f32[12,512,1024]{2,1,0:T(8,128)} %get-tuple-element.433) | copy-start | bytes 75497472 | tf_op jit(solution)/shard_map/while/body/eval_jaxpr/while
  121.9 23.0 %copy-start.9 = (bf16[1024,12,64]{0,2,1:T(8,128)(2,1)S(1)}, bf16[1024,12,64]{0,2,1:T(8,128)(2,1)}, u32[]{:S(2)}) copy-start(bf16[1024,12,64]{0,2,1:T(8,128)(2,1)} %get-tuple-element.479) | copy-start | bytes 4718596 | tf_op jit(solution)/shard_map/while/body/eval_jaxpr/while
  132.6 15.4 %copy-start = (f32[12,512,1024]{2,1,0:T(8,128)S(1)}, f32[12,512,1024]{2,1,0:T(8,128)}, u32[]{:S(2)}) copy-start(f32[12,512,1024]{2,1,0:T(8,128)} %get-tuple-element.433) | copy-start | bytes 75497472 | tf_op jit(solution)/shard_map/while/body/eval_jaxpr/while
  156.5 5.8 copy-start.1
  156.5 5.8 copy-start.7
  156.5 5.8 copy-start.25
  156.5 5.8 copy-start.63
  166.6 43.9 %copy-start.4 = (f32[1024,768]{0,1:T(8,128)}, f32[1024,768]{0,1:T(8,128)S(1)}, u32[]{:S(2)}) copy-start(f32[1024,768]{0,1:T(8,128)S(1)} %get-tuple-element.316) | copy-start | bytes 9437188
  166.6 43.9 %copy-start.27 = (f32[1024]{0:T(1024)}, f32[1024]{0:T(1024)S(1)}, u32[]{:S(2)}) copy-start(f32[1024]{0:T(1024)S(1)} %broadcast_multiply_fusion) | copy-start | bytes 12292
  167.6 42.9 %copy-start.34 = (f32[1024]{0:T(1024)}, f32[1024]{0:T(1024)S(1)}, u32[]{:S(2)}) copy-start(f32[1024]{0:T(1024)S(1)} %fusion.48) | copy-start | bytes 12292
  169.3 20.2 %collective-permute-start = (bf16[1024,768]{0,1:T(8,128)(2,1)}, bf16[1024,768]{0,1:T(8,128)(2,1)}, u32[]{:S(2)}, u32[]{:S(2)}) collective-permute-start(bf16[1024,768]{0,1:T(8,128)(2,1)} %add_convert_fusion.2), channel_id=1, source_target_pairs={{0,1},{1,2},{2,3},{3,0},{4,5},{5,6},{6,7},{7,4},{8,9},{9,10},{10,1... | collective-permute-start | bytes 4718600 | tf_op jit(solution)/shard_map/ppermute | solution.py:161
  169.5 116.7 %all-gather.11.cloned.1.call-start = ((), (), s32[]{:S(2)}) async-start(), calls=%async_computation.8 | async-start | bytes 7864320 | tf_op jit(solution)/shard_map/all_gather | solution.py:180
  189.5 20.2 %collective-permute-start.1 = (bf16[1024,768]{0,1:T(8,128)(2,1)}, bf16[1024,768]{0,1:T(8,128)(2,1)}, u32[]{:S(2)}, u32[]{:S(2)}) collective-permute-start(bf16[1024,768]{0,1:T(8,128)(2,1)} %collective-permute-done), channel_id=1, source_target_pairs={{0,1},{1,2},{2,3},{3,0},{4,5},{5,6},{6,7},{7,4},{8,9},{9,10},{10,1... | collective-permute-start | bytes 4718600 | tf_op jit(solution)/shard_map/ppermute | solution.py:161
  209.6 20.2 %collective-permute-start.2 = (bf16[1024,768]{0,1:T(8,128)(2,1)}, bf16[1024,768]{0,1:T(8,128)(2,1)}, u32[]{:S(2)}, u32[]{:S(2)}) collective-permute-start(bf16[1024,768]{0,1:T(8,128)(2,1)} %collective-permute-done.1), channel_id=1, source_target_pairs={{0,1},{1,2},{2,3},{3,0},{4,5},{5,6},{6,7},{7,4},{8,9},{9,10},{10,1... | collective-permute-start | bytes 4718600 | tf_op jit(solution)/shard_map/ppermute | solution.py:161
  209.6 158.0 %reduce-scatter.7.cloned.1.call-start = ((), (), s32[]{:S(2)}) async-start(), calls=%async_computation.9 | async-start | bytes 7864320 | tf_op jit(solution)/shard_map/reduce_scatter | solution.py:194
  251.6 34.7 %copy-start.65 = (bf16[2,768,768]{2,1,0:T(8,128)(2,1)S(1)}, bf16[2,768,768]{2,1,0:T(8,128)(2,1)}, u32[]{:S(2)}) copy-start(bf16[2,768,768]{2,1,0:T(8,128)(2,1)} %all-gather.9.cloned.1.call-done) | copy-start | bytes 7077892
  311.1 335.8 %reduce-scatter.5.cloned.1.call-start = ((), (), s32[]{:S(2)}) async-start(), calls=%async_computation.7 | async-start | bytes 7864320 | tf_op jit(solution)/shard_map/reduce_scatter | solution.py:171
  324.6 43.1 %copy-start.5 = (f32[1024,768]{0,1:T(8,128)S(1)}, f32[1024,768]{0,1:T(8,128)}, u32[]{:S(2)}) copy-start(f32[1024,768]{0,1:T(8,128)} %copy-done.4) | copy-start | bytes 9437188
  324.6 43.1 %copy-start.28 = (f32[1024]{0:T(1024)S(1)}, f32[1024]{0:T(1024)}, u32[]{:S(2)}) copy-start(f32[1024]{0:T(1024)} %copy-done.27) | copy-start | bytes 12292
  324.6 43.1 %copy-start.31 = (f32[768]{0:T(1024)S(1)}, f32[768]{0:T(1024)}, u32[]{:S(2)}) copy-start(f32[768]{0:T(1024)} %get-tuple-element.247) | copy-start | bytes 9220
  324.6 46.1 %copy-start.46 = (f32[1024]{0:T(1024)S(1)}, f32[1024]{0:T(1024)}, u32[]{:S(2)}) copy-start(f32[1024]{0:T(1024)} %copy-done.45) | copy-start | bytes 12292
  324.6 46.1 %copy-start.35 = (f32[1024]{0:T(1024)S(1)}, f32[1024]{0:T(1024)}, u32[]{:S(2)}) copy-start(f32[1024]{0:T(1024)} %copy-done.34) | copy-start | bytes 12292
  324.6 531.2 %all-reduce.6.cloned.1.call-start = ((), (), s32[]{:S(2)}) async-start(), calls=%async_computation.12 | async-start | bytes 19218432 | tf_op jit(solution)/shard_map/psum | solution.py:254
  381.5 12.2 %copy-start.19 = (bf16[1024,12,64]{0,2,1:T(8,128)(2,1)S(1)}, bf16[1024,12,64]{0,2,1:T(8,128)(2,1)}, u32[]{:S(2)}) copy-start(bf16[1024,12,64]{0,2,1:T(8,128)(2,1)} %get-tuple-element.525) | copy-start | bytes 4718596 | tf_op jit(solution)/shard_map/while/body/eval_jaxpr/while
  446.7 9.5 %copy-start.8 = (bf16[1024,12,64]{0,2,1:T(8,128)(2,1)S(1)}, bf16[1024,12,64]{0,2,1:T(8,128)(2,1)}, u32[]{:S(2)}) copy-start(bf16[1024,12,64]{0,2,1:T(8,128)(2,1)} %get-tuple-element.521) | copy-start | bytes 4718596 | tf_op jit(solution)/shard_map/while/body/eval_jaxpr/while
  468.4 11.5 %copy-start.19 = (bf16[1024,12,64]{0,2,1:T(8,128)(2,1)S(1)}, bf16[1024,12,64]{0,2,1:T(8,128)(2,1)}, u32[]{:S(2)}) copy-start(bf16[1024,12,64]{0,2,1:T(8,128)(2,1)} %get-tuple-element.525) | copy-start | bytes 4718596 | tf_op jit(solution)/shard_map/while/body/eval_jaxpr/while
  533.4 9.5 %copy-start.8 = (bf16[1024,12,64]{0,2,1:T(8,128)(2,1)S(1)}, bf16[1024,12,64]{0,2,1:T(8,128)(2,1)}, u32[]{:S(2)}) copy-start(bf16[1024,12,64]{0,2,1:T(8,128)(2,1)} %get-tuple-element.521) | copy-start | bytes 4718596 | tf_op jit(solution)/shard_map/while/body/eval_jaxpr/while
  557.0 6.6 copy-start.3
  567.5 6.0 copy-start.11
  567.5 6.0 copy-start.39
  567.5 6.0 copy-start.48
  567.5 6.0 copy-start.50
  567.6 6.0 copy-start.61
  618.4 239.2 %reduce-scatter.11.cloned.1.call-start = ((), (), s32[]{:S(2)}) async-start(), calls=%async_computation.11 | async-start | bytes 5308416 | tf_op jit(solution)/shard_map/reduce_scatter | solution.py:202
  639.6 5.5 copy-start.57
  639.6 249.4 %reduce-scatter.9.cloned.1.call-start = ((), (), s32[]{:S(2)}) async-start(), calls=%async_computation.10 | async-start | bytes 2433024 | tf_op jit(solution)/shard_map/reduce_scatter | solution.py:252
  (36 other events, 105.9 us)
Sparse Core Ops, SparseCore 0:
  11.8 62.7 all-gather.4
  77.5 52.6 all-gather.6
  618.5 237.2 all-reduce.5
Sparse Core Ops, SparseCore 1:
  169.6 51.5 all-gather.8
  222.6 44.7 all-gather.10
  311.2 56.4 reduce-scatter.6
  370.2 57.7 reduce-scatter.4
  639.6 129.5 reduce-scatter.10
  775.1 113.9 reduce-scatter.8
